TPU v7x, 32 devices: a whole 2x2x4 slice. The times are simulated.
32 devices in a mesh: seq: 8 (over z, y), chan: 4 (over x, core).
Axes of the slice: x: 2, y: 2, z: 4, core: 2. Of those that a mesh axis runs over, the one named last changes fastest.
Arguments:
- hidden_in: bfloat16 [1024, 2048], P('seq', 'chan'), may hold values from -6 to 6
- norm_gain: float32 [2048], replicated, may hold values from 0.5 to 1.5
- in_weight: bfloat16 [2048, 2, 4096], P('seq', None, 'chan'), may hold values from -0.125 to 0.125
- conv_weight: float32 [2, 4, 4096], P(None, None, 'chan'), may hold values from -3 to 3
- conv_bias: float32 [2, 4096], P(None, 'chan'), may hold values from -0.5 to 0.5
- proj_weight: bfloat16 [2, 4096, 160], P(None, 'chan'), may hold values from -0.1875 to 0.1875
- step_weight: bfloat16 [2, 128, 4096], P(None, None, 'chan'), may hold values from -0.5 to 0.5
- decay_rate: float32 [2, 4096], P(None, 'chan'), may hold values from 0.00024414062 to 0.25
- skip_gain: float32 [2, 4096], P(None, 'chan'), may hold values from 0.5 to 1.5
- out_weight: bfloat16 [4096, 2048], P('chan', 'seq'), may hold values from -0.09375 to 0.09375
Outputs:
- mixed: bfloat16 [1024, 2048], P('seq', 'chan')
All inputs are finite; a program needn't handle non-finite values.
Results may differ from a plain program's by a relative error of at most 0.0095.
Values may be sent and summed in bfloat16 or wider, within the bound.
No kernel may reach another device: no remote copies, remote signals or barrier semaphores. Data moves between devices by JAX's collectives and lax.ppermute only.
A program may use at most 128 MiB of HBM per device.

v0:
```python
import jax
import jax.numpy as jnp
from jax import lax
from jax.sharding import PartitionSpec as P

STATE = 16
WIDTH = 4


def with_halo(block, sides, width):
    for axis, dim in sides:
        count = lax.axis_size(axis)
        forward = [(i, i + 1) for i in range(count - 1)]
        backward = [(target, source) for source, target in forward]
        low = lax.ppermute(
            lax.slice_in_dim(block, block.shape[dim] - width, None, axis=dim), axis, forward
        )
        high = lax.ppermute(lax.slice_in_dim(block, 0, width, axis=dim), axis, backward)
        block = jnp.concatenate([low, block, high], axis=dim)
    return block


def entering(array, axis, combine, identity, reverse):
    devices, here = (lax.axis_size(axis), lax.axis_index(axis))
    everything = jax.tree.map(lambda part: lax.all_gather(part, axis), array)
    start = jax.tree.map(
        lambda part, zero: jnp.broadcast_to(jnp.asarray(zero, part.dtype), part.shape),
        array,
        identity,
    )

    def hop(k, before):
        at = devices - 1 - k if reverse else k
        reached = at > here if reverse else at < here
        new = combine(before, jax.tree.map(lambda part: part[at], everything))
        return jax.tree.map(lambda a, b: jnp.where(reached, a, b), new, before)

    return lax.fori_loop(0, devices, hop, start)


def conv_taps(padded, conv_weight, conv_bias, length):
    reach = conv_weight.shape[1] - 1
    forward = jnp.zeros((length, padded.shape[1]), jnp.float32) + conv_bias[0][None, :]
    backward = jnp.zeros((length, padded.shape[1]), jnp.float32) + conv_bias[1][None, :]
    for offset in range(reach + 1):
        forward = forward + conv_weight[0, offset][None, :] * padded[offset : offset + length]
        begin = 2 * reach - offset
        backward = backward + conv_weight[1, offset][None, :] * padded[begin : begin + length]
    return jax.nn.silu(jnp.stack([forward, backward])).astype(jnp.bfloat16)


def sweep(drive_values, key_rows, query_rows, epsilon, initial, reverse, keeping):
    product = jnp.ones(initial.shape, jnp.float32)

    def advance(carry, current):
        product, state = carry
        drive_row, key_row, query_row, eps_row = current
        decay = 1.0 - eps_row[None, :] * (key_row * key_row)[:, None]
        state = decay * state + key_row[:, None] * (eps_row * drive_row)[None, :]
        product = decay * product
        if keeping == "reads":
            output = jnp.sum(query_row[:, None] * state, axis=0)
        else:
            output = None
        return ((product, state), output)

    (product, state), outputs = lax.scan(
        advance,
        (product, initial),
        (drive_values, key_rows, query_rows, epsilon),
        reverse=reverse,
        unroll=16,
    )
    return (product, state, outputs)


def combine(earlier, latter):
    return (latter[0] * earlier[0], latter[0] * earlier[1] + latter[1])


def per_device(
    hidden_in,
    norm_gain,
    in_weight,
    conv_weight,
    conv_bias,
    proj_weight,
    step_weight,
    decay_rate,
    skip_gain,
    out_weight,
):
    gathered = lax.all_gather(hidden_in, "chan", axis=1, tiled=True).astype(jnp.float32)
    normed = (
        gathered
        * lax.rsqrt(jnp.mean(gathered * gathered, axis=1, keepdims=True) + 1e-05)
        * norm_gain[None, :]
    ).astype(jnp.bfloat16)
    row_count = normed.shape[0]
    channels = in_weight.shape[2]
    piece = lax.all_gather(in_weight, "seq", axis=0, tiled=True)
    projected = jnp.dot(
        normed, piece.reshape(piece.shape[0], 2 * channels), preferred_element_type=jnp.float32
    )
    projected = projected.astype(jnp.bfloat16).reshape(row_count, 2, channels)
    branch = projected[:, 0, :]
    gate_half = projected[:, 1, :].astype(jnp.float32)
    padded = with_halo(branch, (("seq", 0),), WIDTH - 1).astype(jnp.float32)
    driven = conv_taps(padded, conv_weight, conv_bias, row_count)
    partial_value = jnp.einsum(
        "dte,def->tdf", driven, proj_weight, preferred_element_type=jnp.float32
    )
    features = lax.psum(partial_value, "chan")
    key_rows = features[:, :, :STATE]
    query_rows = features[:, :, STATE : 2 * STATE]
    low_rank = features[:, :, 2 * STATE :].astype(jnp.bfloat16)
    step_size = jnp.einsum(
        "tdr,dre->tde", low_rank, step_weight, preferred_element_type=jnp.float32
    )
    beta_rows = 2.0 * decay_rate[None, :, :] * jax.nn.sigmoid(step_size)
    epsilon = beta_rows / (1.0 + beta_rows * jnp.sum(key_rows * key_rows, axis=2, keepdims=True))
    drive_values = driven.astype(jnp.float32)
    zero_state = jnp.zeros((STATE, channels), jnp.float32)
    keeping = "summary"
    passes = [
        sweep(
            drive_values[direction],
            key_rows[:, direction],
            query_rows[:, direction],
            epsilon[:, direction],
            zero_state,
            direction == 1,
            keeping,
        )
        for direction in range(2)
    ]
    identity = (jnp.ones((STATE, channels), jnp.float32), zero_state)
    incoming_forward = entering((passes[0][0], passes[0][1]), "seq", combine, identity, False)[1]
    incoming_reverse = entering((passes[1][0], passes[1][1]), "seq", combine, identity, True)[1]
    incoming = [incoming_forward, incoming_reverse]
    total = jnp.zeros((row_count, channels), jnp.float32)
    for direction in range(2):
        reads = sweep(
            drive_values[direction],
            key_rows[:, direction],
            query_rows[:, direction],
            epsilon[:, direction],
            incoming[direction],
            direction == 1,
            "reads",
        )[2]
        total = total + reads + skip_gain[direction][None, :] * drive_values[direction]
    combined = (total * jax.nn.silu(gate_half)).astype(jnp.bfloat16)
    partial_out = jnp.dot(
        combined,
        lax.all_gather(out_weight, "seq", axis=1, tiled=True),
        preferred_element_type=jnp.float32,
    )
    summed = lax.psum(partial_out, "chan")
    share_width = summed.shape[1] // lax.axis_size("chan")
    share = lax.dynamic_slice_in_dim(summed, lax.axis_index("chan") * share_width, share_width, 1)
    return share.astype(jnp.bfloat16)


def solution(mesh):
    in_specs = (
        P("seq", "chan"),
        P(),
        P("seq", None, "chan"),
        P(None, None, "chan"),
        P(None, "chan"),
        P(None, "chan", None),
        P(None, None, "chan"),
        P(None, "chan"),
        P(None, "chan"),
        P("chan", "seq"),
    )
    out_specs = P("seq", "chan")
    return jax.shard_map(
        per_device, mesh=mesh, in_specs=in_specs, out_specs=out_specs, check_vma=False
    )
```

profile of v0, /device:TPU:0, one launch (start us, length us, event | category | flops | bytes accessed | tf_op | source)
XLA Modules:
  0.0 489.7 jit_solution(10717089666315897083)
XLA Ops:
  7.3 8.9 %all_gather.33 = bf16[128,2048]{1,0:T(8,128)(2,1)S(1)} all-gather(bf16[128,512]{1,0:T(8,128)(2,1)} %param.22), channel_id=1, replica_groups=mesh['seq'=8,'chan'=4] {'chan'}, dimensions={1}, use_global_device_ids=true | all-gather | bytes 655360 | tf_op jit(solution)/shard_map/all_gather | solution.py:93
  18.1 118.6 %all-gather.7.cloned.1.call-done = bf16[2048,2,1024]{2,1,0:T(2,128)(2,1)} async-done(((bf16[256,2,1024]{2,1,0:T(2,128)(2,1)}), bf16[2048,2,1024]{2,1,0:T(2,128)(2,1)}) %all-gather.7.cloned.1.call-update) | async-done | bytes 8388624 | tf_op jit(solution)/shard_map/all_gather | solution.py:101
  136.7 10.1 %copy.42 = bf16[256,8,2,1024]{3,1,2,0:T(8,128)(2,1)} copy(bf16[256,8,2,1024]{3,2,1,0:T(2,128)(2,1)} %bitcast.855) | data formatting | bytes 16777216
  146.8 4.7 convolution_convert_fusion
  152.0 1.3 collective-permute-start.1
  153.3 4.5 collective-permute-start
  157.8 1.5 fusion.335
  163.2 30.7 %all-reduce.3.cloned.1.call-done = f32[128,2,160]{0,2,1:T(8,128)} async-done(((f32[128,2,160]{0,2,1:T(8,128)}), f32[128,2,160]{0,2,1:T(8,128)}) %all-reduce.3.cloned.1.call-update) | async-done | bytes 163856 | tf_op jit(solution)/shard_map/psum | solution.py:113
  196.4 1.7 add_divide_fusion
  199.1 22.7 %while.92 = (s32[]{:T(128)}, f32[16,1024]{1,0:T(8,128)S(1)}, f32[16,1024]{1,0:T(8,128)S(1)}, f32[8,16,1024]{2,1,0:T(8,128)}, f32[8,16,16]{2,1,0:T(8,128)S(1)}, /...) while((s32[]{:T(128)}, f32[16,1024]{1,0:T(8,128)S(1)}, ...), condition=%wide.region_26.27_spmd.clone, body=%wide.region_25.26_spmd.clone.sunk | while | flops 2146579 | bytes 924200 | solution.py:67
  199.1 2.0 constant_dynamic-slice_fusion.231
  202.1 2.0 constant_dynamic-slice_fusion.231
  205.1 1.8 constant_dynamic-slice_fusion.231
  207.8 1.8 constant_dynamic-slice_fusion.231
  210.6 2.0 constant_dynamic-slice_fusion.231
  213.5 2.0 constant_dynamic-slice_fusion.231
  216.5 1.8 constant_dynamic-slice_fusion.231
  219.2 1.8 constant_dynamic-slice_fusion.231
  221.8 9.5 %while.90 = (s32[]{:T(128)}, f32[16,1024]{1,0:T(8,128)S(1)}, f32[16,1024]{1,0:T(8,128)S(1)}, f32[8,16,1024]{2,1,0:T(8,128)S(1)}, f32[8,16,16]{2,1,0:T(8,128)S(1)...) while((s32[]{:T(128)}, f32[16,1024]{1,0:T(8,128)S(1)}, ...), condition=%wide.region_4.5_spmd.clone, body=%wide.region_3.4_spmd.clone.sunk | while | flops 2146578 | bytes 924180 | solution.py:67
  231.3 37.0 %all-gather.1 = f32[128,1024]{1,0:T(8,128)} all-gather(f32[16,1024]{1,0:T(8,128)S(1)} %get-tuple-element.566), channel_id=3, replica_groups=mesh['seq'=8,'chan'=4] {'seq'}, dimensions={0}, use_global_device_ids=true | all-gather | bytes 589824 | tf_op jit(solution)/shard_map/all_gather | solution.py:25
  268.3 34.7 %all-gather.3 = f32[128,1024]{1,0:T(8,128)} all-gather(f32[16,1024]{1,0:T(8,128)S(1)} %get-tuple-element.570), channel_id=5, replica_groups=mesh['seq'=8,'chan'=4] {'seq'}, dimensions={0}, use_global_device_ids=true | all-gather | bytes 589824 | tf_op jit(solution)/shard_map/all_gather | solution.py:25
  303.0 33.4 %all-gather = f32[128,1024]{1,0:T(8,128)} all-gather(f32[16,1024]{1,0:T(8,128)S(1)} %get-tuple-element.565), channel_id=2, replica_groups=mesh['seq'=8,'chan'=4] {'seq'}, dimensions={0}, use_global_device_ids=true | all-gather | bytes 589824 | tf_op jit(solution)/shard_map/all_gather | solution.py:25
  336.4 7.5 %while.91 = (s32[]{:T(128)}, f32[16,1024]{1,0:T(8,128)S(1)}, s32[]{:T(128)}, f32[8,16,1024]{2,1,0:T(8,128)}, f32[8,16,1024]{2,1,0:T(8,128)}, /*index=5*/s32[]{:T(128)}, s32[]{:T(128)}) while((s32[]{:T(128)}, f32[16,1024]{1,0:T(8,128)S(1)}, s32[]{:T(128)}, f32[8,16,1024]{2,1,0:T(8,128)}, f32[8,16,1024]{2,1,0:T(8,128)}, ...), condition=%wide.region_6.7_spmd.clone, body=%wide.region_5.6_spmd.clone.sunk | while | flops 65540 | bytes 262253 | solution.py:38
  343.9 33.6 %all-gather.2 = f32[128,1024]{1,0:T(8,128)} all-gather(f32[16,1024]{1,0:T(8,128)S(1)} %get-tuple-element.569), channel_id=4, replica_groups=mesh['seq'=8,'chan'=4] {'seq'}, dimensions={0}, use_global_device_ids=true | all-gather | bytes 589824 | tf_op jit(solution)/shard_map/all_gather | solution.py:25
  377.5 7.5 %while.93 = (s32[]{:T(128)}, f32[16,1024]{1,0:T(8,128)S(1)}, s32[]{:T(128)}, f32[8,16,1024]{2,1,0:T(8,128)}, f32[8,16,1024]{2,1,0:T(8,128)}, /*index=5*/s32[]{:T(128)}, s32[]{:T(128)}, s32[]{:T(128)}, s32[]{:T(128)}) while((s32[]{:T(128)}, f32[16,1024]{1,0:T(8,128)S(1)}, s32[]{:T(128)}, f32[8,16,1024]{2,1,0:T(8,128)}, ...), condition=%wide.region_28.29_spmd.clone, body=%wide.region_27.28_spmd.clone.sunk | while | flops 65544 | bytes 262315 | solution.py:38
  385.9 33.0 %while.89 = (s32[]{:T(128)}, f32[16,1024]{1,0:T(8,128)S(1)}, f32[8,16,1024]{2,1,0:T(8,128)}, f32[8,16,1024]{2,1,0:T(8,128)}, f32[8,16,16]{2,1,0:T(8,128)S(1)}, /...) while((s32[]{:T(128)}, f32[16,1024]{1,0:T(8,128)S(1)}, ...), condition=%wide.region_46.47_spmd, body=%wide.region_29.46_spmd.sunk | while | flops 2408722 | bytes 2033121 | solution.py:67
  386.1 2.0 constant_dynamic-slice_fusion.229
  390.3 2.0 constant_dynamic-slice_fusion.229
  394.6 1.8 constant_dynamic-slice_fusion.229
  398.6 1.8 constant_dynamic-slice_fusion.229
  402.6 2.0 constant_dynamic-slice_fusion.229
  406.8 2.0 constant_dynamic-slice_fusion.229
  411.0 1.8 constant_dynamic-slice_fusion.229
  415.0 1.8 constant_dynamic-slice_fusion.229
  418.9 32.4 %while.88 = (s32[]{:T(128)}, f32[16,1024]{1,0:T(8,128)S(1)}, f32[8,16,1024]{2,1,0:T(8,128)S(1)}, f32[8,16,1024]{2,1,0:T(8,128)S(1)}, f32[8,16,16]{2,1,0:T(8,128)...) while((s32[]{:T(128)}, f32[16,1024]{1,0:T(8,128)S(1)}, ...), condition=%wide.region_24.25_spmd, body=%wide.region_7.24_spmd.sunk | while | flops 2490641 | bytes 2106965 | solution.py:67
  420.0 1.1 fusion.360
  424.0 1.1 fusion.360
  428.0 1.1 fusion.360
  431.0 1.1 fusion.359
  432.1 1.1 fusion.360
  436.1 1.1 fusion.360
  440.2 1.1 fusion.360
  444.2 1.1 fusion.360
  447.2 1.1 fusion.359
  448.3 1.1 fusion.360
  451.3 1.5 fusion.203
  452.8 2.9 fusion.342
  455.7 26.7 %all-reduce.4 = bf16[128,2048]{1,0:T(8,128)(2,1)S(1)} all-reduce(f32[128,2048]{1,0:T(8,128)S(1)} %fusion.342), channel_id=1, replica_groups=mesh['seq'=8,'chan'=4] {'chan'}, use_global_device_ids=true, to_apply=%region_47.48 | all-reduce | flops 262144 | bytes 1572864 | tf_op jit(solution)/shard_map/psum | solution.py:159
  (837 shorter events, 76.6 us)
Async XLA Ops:
  6.5 153.8 %copy-start = (bf16[2,1024,160]{1,2,0:T(8,128)(2,1)S(1)}, bf16[2,1024,160]{1,2,0:T(8,128)(2,1)}, u32[]{:S(2)}) copy-start(bf16[2,1024,160]{1,2,0:T(8,128)(2,1)} %param.27) | copy-start | bytes 1966084
  6.5 130.2 %all-gather.7.cloned.1.call-start = ((), (), s32[]{:S(2)}) async-start(), calls=%async_computation | async-start | bytes 9437184 | tf_op jit(solution)/shard_map/all_gather | solution.py:101
  7.3 186.6 %all-reduce.3.cloned.1.call-start = ((), (), s32[]{:S(2)}) async-start(), calls=%async_computation.1 | async-start | bytes 327680 | tf_op jit(solution)/shard_map/psum | solution.py:113
  136.7 10.1 %copy-start.4 = (f32[2048]{0:T(1024)S(1)}, f32[2048]{0:T(1024)}, u32[]{:S(2)}) copy-start(f32[2048]{0:T(1024)} %param.23) | copy-start | bytes 24580
  151.5 10.6 %copy-start.5 = (f32[2,1024]{1,0:T(2,128)S(1)}, f32[2,1024]{1,0:T(2,128)}, u32[]{:S(2)}) copy-start(f32[2,1024]{1,0:T(2,128)} %param.29) | copy-start | bytes 24580
  151.5 10.7 %copy-start.6 = (f32[2,1024]{1,0:T(2,128)S(1)}, f32[2,1024]{1,0:T(2,128)}, u32[]{:S(2)}) copy-start(f32[2,1024]{1,0:T(2,128)} %param.30) | copy-start | bytes 24580
  152.0 7.5 %collective-permute-start.1 = (bf16[3,1024]{1,0:T(4,128)(2,1)S(1)}, bf16[3,1024]{1,0:T(4,128)(2,1)S(1)}, u32[]{:S(2)}, u32[]{:S(2)}) collective-permute-start(bf16[3,1024]{1,0:T(4,128)(2,1)S(1)} %bitcast.1151), channel_id=1, source_target_pairs={{4,0},{8,4},{12,8},{16,12},{20,16},{24,20},{28,24},{5,1},{9,5},{13... | collective-permute-start | bytes 18440 | tf_op jit(solution)/shard_map/ppermute | solution.py:18
  153.3 6.2 %collective-permute-start = (bf16[3,1024]{1,0:T(4,128)(2,1)S(1)}, bf16[3,1024]{1,0:T(4,128)(2,1)S(1)}, u32[]{:S(2)}, u32[]{:S(2)}) collective-permute-start(bf16[3,1024]{1,0:T(4,128)(2,1)S(1)} %bitcast.1150), channel_id=1, source_target_pairs={{0,4},{4,8},{8,12},{12,16},{16,20},{20,24},{24,28},{1,5},{5,9},{9,... | collective-permute-start | bytes 18440 | tf_op jit(solution)/shard_map/ppermute | solution.py:15
  161.4 291.4 %all-gather.9.cloned.1.call-start = ((), (), s32[]{:S(2)}) async-start(), calls=%async_computation.2 | async-start | bytes 4718592 | tf_op jit(solution)/shard_map/all_gather | solution.py:156
  163.2 35.9 %copy-start.1 = (f32[16,1024]{1,0:T(8,128)S(1)}, f32[16,1024]{1,0:T(8,128)}, u32[]{:S(2)}) copy-start(f32[16,1024]{1,0:T(8,128)} %custom-call.4) | copy-start | bytes 196612
  163.2 35.9 %copy-start.2 = (f32[16,1024]{1,0:T(8,128)S(1)}, f32[16,1024]{1,0:T(8,128)}, u32[]{:S(2)}) copy-start(f32[16,1024]{1,0:T(8,128)} %custom-call.3) | copy-start | bytes 196612
  231.3 154.6 %copy-start.3 = (f32[8,16,16]{2,1,0:T(8,128)}, f32[8,16,16]{2,1,0:T(8,128)S(1)}, u32[]{:S(2)}) copy-start(f32[8,16,16]{2,1,0:T(8,128)S(1)} %get-tuple-element.2563) | copy-start | bytes 24580
Sparse Core Ops, SparseCore 0:
  9.5 127.1 all-gather.6
  161.5 32.3 all-reduce.2
  195.9 86.4 all-gather.8
where the time goes:
time: 494 us; the launch traced here: 490 us
  blocking collectives  174 us (35%)
  waiting for transfers between devices  151 us (31%)
  local copies, waits for them, and re-layouts  69.2 us (14%)
  other arithmetic  59.8 us (12%)
  between operations  13.4 us (3%)
  matrix products  10.3 us (2%)
  loops' own time  6.06 us (1%)
  starting transfers between devices  5.92 us (1%)
    all_gather x4, blocking collectives, entering(): everything = jax.tree.map(lambda part: lax.all_gather(part, axis), array)  139 us
    all_gather x1, waiting for transfers between devices, per_device(): piece = lax.all_gather(in_weight, 'seq', axis=0, tiled=True)  119 us
    slice x32, local copies, waits for them, and re-layouts, sweep(): lax.scan(advance, (product, initial), (drive_values, key_rows, query_rows...  34.3 us
    psum x1, waiting for transfers between devices, per_device(): features = lax.psum(partial_value, 'chan')  30.7 us
    psum x1, blocking collectives, per_device(): summed = lax.psum(partial_out, 'chan')  26.7 us
    reduce_sum x136, other arithmetic, advance(): output = jnp.sum(query_row[:, None] * state, axis=0)  17.7 us
    select_n x16, other arithmetic, hop(): return jax.tree.map(lambda a, b: jnp.where(reached, a, b), new, before)  14.6 us
    mul x32, other arithmetic, advance(): decay = 1.0 - eps_row[None, :] * (key_row * key_row)[:, None]  12.7 us
  transfers between devices with their start and end apart: 5, of which 2 were waited for; matrix products, arithmetic and copies ran while one was open for 24% of the time, Pallas kernels for 0%

commit v1 on v0

--- a/solution.py
+++ b/solution.py
@@ -110,7 +110,11 @@
     partial_value = jnp.einsum(
         "dte,def->tdf", driven, proj_weight, preferred_element_type=jnp.float32
     )
-    features = lax.psum(partial_value, "chan")
+    features = partial_value
+    for hop_ in (1, 2):
+        features = features + lax.ppermute(
+            features, "chan", [(dev, dev ^ hop_) for dev in range(4)]
+        )
     key_rows = features[:, :, :STATE]
     query_rows = features[:, :, STATE : 2 * STATE]
     low_rank = features[:, :, 2 * STATE :].astype(jnp.bfloat16)

time: 494 us -> 510 us (1.032)
  other arithmetic: 59.8 us -> 103 us
  waiting for transfers between devices: 151 us -> 125 us
    psum x1 -> x0, waiting for transfers between devices: 30.7 us -> none  [per_device(): features = lax.psum(partial_value, 'chan')]
    mul x32, other arithmetic: 12.7 us -> 34.5 us  [advance(): decay = 1.0 - eps_row[None, :] * (key_row * key_row)[:, None]]
    add x16, other arithmetic: 5.87 us -> 16.9 us  [advance(): state = decay * state + key_row[:, None] * (eps_row * drive_row)[None, :]]
    mul x16, other arithmetic: 3.1 us -> 13.9 us  [advance(): product = decay * product]
    mul x16, local copies, waits for them, and re-layouts: 8.66 us -> 16.3 us  [advance(): output = jnp.sum(query_row[:, None] * state, axis=0)]
    slice x32, local copies, waits for them, and re-layouts: 34.3 us -> 27.3 us  [sweep(): lax.scan(advance, (product, initial), (drive_values, key_rows, query_rows...]
    ppermute x0 -> x2, waiting for transfers between devices: none -> 5.97 us  [per_device(): lax.ppermute(features, 'chan', [(dev, dev ^ hop_) for dev in range(4)])]
    unnamed x20 -> x12, local copies, waits for them, and re-layouts: 10.5 us -> 11.7 us
  transfers between devices with their start and end apart: 5 -> 6, of which waited for: 2 -> 3; matrix products, arithmetic and copies ran while one was open for 24% -> 36% of each run, Pallas kernels for 0% -> 0%
where the time goes in v1:
time: 510 us; the launch traced here: 504 us
  blocking collectives  169 us (33%)
  waiting for transfers between devices  125 us (25%)
  other arithmetic  103 us (20%)
  local copies, waits for them, and re-layouts  70.1 us (14%)
  between operations  13.7 us (3%)
  matrix products  9.6 us (2%)
  starting transfers between devices  7.54 us (1%)
  loops' own time  5.76 us (1%)
    all_gather x4, blocking collectives, entering(): everything = jax.tree.map(lambda part: lax.all_gather(part, axis), array)  135 us
    all_gather x1, waiting for transfers between devices, per_device(): piece = lax.all_gather(in_weight, 'seq', axis=0, tiled=True)  117 us
    mul x32, other arithmetic, advance(): decay = 1.0 - eps_row[None, :] * (key_row * key_row)[:, None]  34.5 us
    slice x32, local copies, waits for them, and re-layouts, sweep(): lax.scan(advance, (product, initial), (drive_values, key_rows, query_rows...  27.3 us
    psum x1, blocking collectives, per_device(): summed = lax.psum(partial_out, 'chan')  25.2 us
    reduce_sum x136, other arithmetic, advance(): output = jnp.sum(query_row[:, None] * state, axis=0)  17.7 us
    add x16, other arithmetic, advance(): state = decay * state + key_row[:, None] * (eps_row * drive_row)[None, :]  16.9 us
    mul x16, local copies, waits for them, and re-layouts, advance(): output = jnp.sum(query_row[:, None] * state, axis=0)  16.3 us
  transfers between devices with their start and end apart: 6, of which 3 were waited for; matrix products, arithmetic and copies ran while one was open for 36% of the time, Pallas kernels for 0%

profile of v1, /device:TPU:0, one launch (start us, length us, event | category | flops | bytes accessed | tf_op | source)
XLA Modules:
  0.0 504.0 jit_solution(11889414719738010851)
XLA Ops:
  10.5 8.9 %all_gather.33 = bf16[128,2048]{1,0:T(8,128)(2,1)S(1)} all-gather(bf16[128,512]{1,0:T(8,128)(2,1)} %param.22), channel_id=1, replica_groups=mesh['seq'=8,'chan'=4] {'chan'}, dimensions={1}, use_global_device_ids=true | all-gather | bytes 655360 | tf_op jit(solution)/shard_map/all_gather | solution.py:93
  19.6 117.1 %all-gather.7.cloned.1.call-done = bf16[2048,2,1024]{2,1,0:T(2,128)(2,1)} async-done(((bf16[256,2,1024]{2,1,0:T(2,128)(2,1)}), bf16[2048,2,1024]{2,1,0:T(2,128)(2,1)}) %all-gather.7.cloned.1.call-update) | async-done | bytes 8388624 | tf_op jit(solution)/shard_map/all_gather | solution.py:101
  136.7 10.1 %copy.42 = bf16[256,8,2,1024]{3,1,2,0:T(8,128)(2,1)} copy(bf16[256,8,2,1024]{3,2,1,0:T(2,128)(2,1)} %bitcast.855) | data formatting | bytes 16777216
  146.8 4.7 convolution_convert_fusion
  153.3 4.5 collective-permute-start
  157.8 1.5 fusion.335
  162.2 1.6 collective-permute-start.3
  163.9 4.6 collective-permute-done.3
  171.4 1.7 add_divide_fusion
  174.0 47.6 %while.92 = (s32[]{:T(128)}, f32[16,1024]{1,0:T(8,128)}, f32[16,1024]{1,0:T(8,128)}, f32[8,16,1024]{2,1,0:T(8,128)}, f32[8,16,16]{2,1,0:T(8,128)}, /*index=5*/f3...) while((s32[]{:T(128)}, f32[16,1024]{1,0:T(8,128)}, ...), condition=%wide.region_25.26_spmd.clone, body=%wide.region_24.25_spmd.clone.sunk | while | flops 2146579 | bytes 924200 | solution.py:67
  175.0 1.5 constant_dynamic-slice_fusion.231
  179.5 1.5 constant_dynamic-slice_fusion.231
  181.1 1.9 multiply_add_fusion.53
  183.0 1.6 fusion.367
  185.6 1.5 constant_dynamic-slice_fusion.231
  187.3 1.9 multiply_add_fusion.53
  189.2 1.6 fusion.367
  191.8 1.5 constant_dynamic-slice_fusion.231
  193.5 1.9 multiply_add_fusion.53
  195.3 1.6 fusion.367
  198.0 1.5 constant_dynamic-slice_fusion.231
  199.6 1.9 multiply_add_fusion.53
  201.5 1.6 fusion.367
  204.1 1.5 constant_dynamic-slice_fusion.231
  205.8 1.9 multiply_add_fusion.53
  207.6 1.6 fusion.367
  210.3 1.5 constant_dynamic-slice_fusion.231
  211.9 1.9 multiply_add_fusion.53
  213.8 1.6 fusion.367
  216.4 1.5 constant_dynamic-slice_fusion.231
  218.1 1.9 multiply_add_fusion.53
  220.0 1.6 fusion.367
  221.6 17.0 %while.90 = (s32[]{:T(128)}, f32[16,1024]{1,0:T(8,128)S(1)}, f32[16,1024]{1,0:T(8,128)S(1)}, f32[8,16,1024]{2,1,0:T(8,128)S(1)}, f32[8,16,16]{2,1,0:T(8,128)}, /...) while((s32[]{:T(128)}, f32[16,1024]{1,0:T(8,128)S(1)}, ...), condition=%wide.region_3.4_spmd.clone, body=%wide.region_2.3_spmd.clone.sunk | while | flops 2146578 | bytes 924180 | solution.py:67
  238.6 34.6 %all-gather.1 = f32[128,1024]{1,0:T(8,128)} all-gather(f32[16,1024]{1,0:T(8,128)S(1)} %get-tuple-element.566), channel_id=3, replica_groups=mesh['seq'=8,'chan'=4] {'seq'}, dimensions={0}, use_global_device_ids=true | all-gather | bytes 589824 | tf_op jit(solution)/shard_map/all_gather | solution.py:25
  273.2 33.7 %all-gather.3 = f32[128,1024]{1,0:T(8,128)} all-gather(f32[16,1024]{1,0:T(8,128)} %get-tuple-element.570), channel_id=5, replica_groups=mesh['seq'=8,'chan'=4] {'seq'}, dimensions={0}, use_global_device_ids=true | all-gather | bytes 589824 | tf_op jit(solution)/shard_map/all_gather | solution.py:25
  306.9 33.6 %all-gather = f32[128,1024]{1,0:T(8,128)} all-gather(f32[16,1024]{1,0:T(8,128)S(1)} %get-tuple-element.565), channel_id=2, replica_groups=mesh['seq'=8,'chan'=4] {'seq'}, dimensions={0}, use_global_device_ids=true | all-gather | bytes 589824 | tf_op jit(solution)/shard_map/all_gather | solution.py:25
  340.5 7.5 %while.91 = (s32[]{:T(128)}, f32[16,1024]{1,0:T(8,128)S(1)}, s32[]{:T(128)}, f32[8,16,1024]{2,1,0:T(8,128)}, f32[8,16,1024]{2,1,0:T(8,128)}, /*index=5*/s32[]{:T(128)}, s32[]{:T(128)}) while((s32[]{:T(128)}, f32[16,1024]{1,0:T(8,128)S(1)}, s32[]{:T(128)}, f32[8,16,1024]{2,1,0:T(8,128)}, f32[8,16,1024]{2,1,0:T(8,128)}, ...), condition=%wide.region_5.6_spmd.clone, body=%wide.region_4.5_spmd.clone.sunk | while | flops 65540 | bytes 262253 | solution.py:38
  348.0 33.4 %all-gather.2 = f32[128,1024]{1,0:T(8,128)} all-gather(f32[16,1024]{1,0:T(8,128)} %get-tuple-element.569), channel_id=4, replica_groups=mesh['seq'=8,'chan'=4] {'seq'}, dimensions={0}, use_global_device_ids=true | all-gather | bytes 589824 | tf_op jit(solution)/shard_map/all_gather | solution.py:25
  381.4 7.5 %while.93 = (s32[]{:T(128)}, f32[16,1024]{1,0:T(8,128)S(1)}, s32[]{:T(128)}, f32[8,16,1024]{2,1,0:T(8,128)}, f32[8,16,1024]{2,1,0:T(8,128)}, /*index=5*/s32[]{:T(128)}, s32[]{:T(128)}, s32[]{:T(128)}, s32[]{:T(128)}) while((s32[]{:T(128)}, f32[16,1024]{1,0:T(8,128)S(1)}, s32[]{:T(128)}, f32[8,16,1024]{2,1,0:T(8,128)}, ...), condition=%wide.region_27.28_spmd.clone, body=%wide.region_26.27_spmd.clone.sunk | while | flops 65544 | bytes 262315 | solution.py:38
  389.8 44.7 %while.89 = (s32[]{:T(128)}, f32[16,1024]{1,0:T(8,128)S(1)}, f32[8,16,1024]{2,1,0:T(8,128)}, f32[8,16,1024]{2,1,0:T(8,128)}, f32[8,16,16]{2,1,0:T(8,128)}, /*ind...) while((s32[]{:T(128)}, f32[16,1024]{1,0:T(8,128)S(1)}, ...), condition=%wide.region_45.46_spmd, body=%wide.region_28.45_spmd.sunk | while | flops 2408722 | bytes 2033121 | solution.py:67
  391.9 1.5 constant_dynamic-slice_fusion.229
  397.5 1.5 constant_dynamic-slice_fusion.229
  403.1 1.5 constant_dynamic-slice_fusion.229
  419.9 1.5 constant_dynamic-slice_fusion.229
  434.5 32.3 %while.88 = (s32[]{:T(128)}, f32[16,1024]{1,0:T(8,128)S(1)}, f32[8,16,1024]{2,1,0:T(8,128)S(1)}, f32[8,16,1024]{2,1,0:T(8,128)S(1)}, f32[8,16,16]{2,1,0:T(8,128)...) while((s32[]{:T(128)}, f32[16,1024]{1,0:T(8,128)S(1)}, ...), condition=%wide.region_23.24_spmd, body=%wide.region_6.23_spmd.sunk | while | flops 2490641 | bytes 2106965 | solution.py:67
  466.8 1.5 fusion.203
  468.4 2.9 fusion.342
  471.3 25.2 %all-reduce.1 = bf16[128,2048]{1,0:T(8,128)(2,1)S(1)} all-reduce(f32[128,2048]{1,0:T(8,128)S(1)} %fusion.342), channel_id=1, replica_groups=mesh['seq'=8,'chan'=4] {'chan'}, use_global_device_ids=true, to_apply=%region_46.47 | all-reduce | flops 262144 | bytes 1572864 | tf_op jit(solution)/shard_map/psum | solution.py:163
  (832 shorter events, 122.7 us)
Async XLA Ops:
  6.5 153.8 %copy-start = (bf16[2,1024,160]{1,2,0:T(8,128)(2,1)S(1)}, bf16[2,1024,160]{1,2,0:T(8,128)(2,1)}, u32[]{:S(2)}) copy-start(bf16[2,1024,160]{1,2,0:T(8,128)(2,1)} %param.27) | copy-start | bytes 1966084
  6.5 130.2 %all-gather.7.cloned.1.call-start = ((), (), s32[]{:S(2)}) async-start(), calls=%async_computation | async-start | bytes 9437184 | tf_op jit(solution)/shard_map/all_gather | solution.py:101
  7.3 461.1 %all-gather.9.cloned.1.call-start = ((), (), s32[]{:S(2)}) async-start(), calls=%async_computation.1 | async-start | bytes 4718592 | tf_op jit(solution)/shard_map/all_gather | solution.py:160
  136.7 10.1 %copy-start.1 = (f32[2048]{0:T(1024)S(1)}, f32[2048]{0:T(1024)}, u32[]{:S(2)}) copy-start(f32[2048]{0:T(1024)} %param.23) | copy-start | bytes 24580
  151.5 9.2 %copy-start.2 = (f32[2,1024]{1,0:T(2,128)S(1)}, f32[2,1024]{1,0:T(2,128)}, u32[]{:S(2)}) copy-start(f32[2,1024]{1,0:T(2,128)} %param.30) | copy-start | bytes 24580
  152.0 7.5 %collective-permute-start.1 = (bf16[3,1024]{1,0:T(4,128)(2,1)S(1)}, bf16[3,1024]{1,0:T(4,128)(2,1)S(1)}, u32[]{:S(2)}, u32[]{:S(2)}) collective-permute-start(bf16[3,1024]{1,0:T(4,128)(2,1)S(1)} %bitcast.1153), channel_id=1, source_target_pairs={{4,0},{8,4},{12,8},{16,12},{20,16},{24,20},{28,24},{5,1},{9,5},{13... | collective-permute-start | bytes 18440 | tf_op jit(solution)/shard_map/ppermute | solution.py:18
  153.3 6.2 %collective-permute-start = (bf16[3,1024]{1,0:T(4,128)(2,1)S(1)}, bf16[3,1024]{1,0:T(4,128)(2,1)S(1)}, u32[]{:S(2)}, u32[]{:S(2)}) collective-permute-start(bf16[3,1024]{1,0:T(4,128)(2,1)S(1)} %bitcast.1152), channel_id=1, source_target_pairs={{0,4},{4,8},{8,12},{12,16},{16,20},{20,24},{24,28},{1,5},{5,9},{9,... | collective-permute-start | bytes 18440 | tf_op jit(solution)/shard_map/ppermute | solution.py:15
  160.7 1.5 collective-permute-start.2
  162.2 6.3 %collective-permute-start.3 = (f32[128,2,160]{0,2,1:T(8,128)S(1)}, f32[128,2,160]{0,2,1:T(8,128)S(1)}, u32[]{:S(2)}, u32[]{:S(2)}) collective-permute-start(f32[128,2,160]{0,2,1:T(8,128)S(1)} %add.591), channel_id=1, source_target_pairs={{0,2},{1,3},{2,0},{3,1},{4,6},{5,7},{6,4},{7,5},{8,10},{9,11},{10,... | collective-permute-start | bytes 491528 | tf_op jit(solution)/shard_map/ppermute | solution.py:115
Sparse Core Ops, SparseCore 0:
  9.5 127.1 all-gather.6
  138.7 72.7 all-gather.8
